TPU v7x, 32 devices: a whole 2x2x4 slice. The times are simulated.
32 devices in a mesh: grp: 2 (over y), seq: 8 (over z, x), tp: 2 (over core).
Axes of the slice: x: 2, y: 2, z: 4, core: 2. Of those that a mesh axis runs over, the one named last changes fastest.
Arguments:
- hidden: bfloat16 [8, 8192], P('grp', 'seq'), parts along dimension 0, may hold values from -40 to 40
- norm_gain: float32 [8192], P('seq'), may hold values from 0.25 to 1.75
- query_proj: bfloat16 [8192, 4096], P('seq', 'tp'), may hold values from -0.0625 to 0.0625
- keyval_proj: bfloat16 [8192, 2, 512], P('seq', None, 'tp'), may hold values from -0.0625 to 0.0625
- attend_proj: bfloat16 [4096, 8192], P('tp', 'seq'), may hold values from -0.09375 to 0.09375
- keyval_cache: bfloat16 [2, 8, 512, 512], P(None, 'grp', 'seq', 'tp'), parts along dimension 1, may hold values from -320 to 320
- lengths: int32 [8], P('grp'), parts along dimension 0, may hold values from 1 to 512, as said below
Outputs:
- hidden_out: bfloat16 [8, 8192], P('grp', 'seq'), parts along dimension 0
- new_keyval: bfloat16 [8, 2, 512], P('grp', None, 'tp'), parts along dimension 0
There are 2 independent parts, one for each index of `grp`. A program takes and returns all parts, laid end to end along the dimension named above; an argument that names none is the same for every part. Nothing has to cross between parts.
Inputs may be any that keep to these rules, and one draw needn't show every extreme that they name: `lengths`: live cached positions of each request; in every draw some request has all 512.
All inputs are finite; a program needn't handle non-finite values.
Results may differ from a plain program's by a relative error of at most 0.0087.
Values sent between devices are 32-bit elements; how exact they have to be, the bound alone decides.
A program may use at most 64 MiB of HBM per device.

v0:
```python
import jax
import jax.numpy as jnp
from jax import lax
from jax.sharding import PartitionSpec as P

D = 8192
HEAD_DIM = 128


EPSILON = 1e-05
MASKED = -1e30


def on_device(hidden, norm_gain, query_proj, keyval_proj, attend_proj, keyval_cache, lengths):
    row_count = hidden.shape[0]
    feature_dev = hidden.shape[1]
    seq_rank = lax.axis_index("seq")
    ctx_dev = keyval_cache.shape[2]
    kv_width = keyval_cache.shape[3]
    kv_heads = kv_width // HEAD_DIM
    q_heads = query_proj.shape[1] // HEAD_DIM
    group_share = q_heads // kv_heads
    score_scale = HEAD_DIM ** (-0.5)
    one_float = hidden.astype(jnp.float32)
    scaled = (one_float * norm_gain).astype(jnp.bfloat16)
    squares = jnp.sum(one_float * one_float, axis=1)
    query_part = jnp.dot(scaled, query_proj, preferred_element_type=jnp.float32)
    keyval_part = jnp.dot(
        scaled, keyval_proj.reshape(feature_dev, 2 * kv_width), preferred_element_type=jnp.float32
    ).reshape(row_count, 2, kv_width)
    query_sum, keyval_sum, squares_sum = lax.psum((query_part, keyval_part, squares), "seq")
    scale_two = lax.rsqrt(squares_sum / D + EPSILON)[:, None]
    query = (query_sum * scale_two).astype(jnp.bfloat16)
    new_keyval = (keyval_sum * scale_two[:, :, None]).astype(jnp.bfloat16)
    query_heads = query.reshape(row_count, kv_heads, group_share, HEAD_DIM)
    cache_keys = keyval_cache[0].reshape(row_count, ctx_dev, kv_heads, HEAD_DIM)
    cache_values = keyval_cache[1].reshape(row_count, ctx_dev, kv_heads, HEAD_DIM)
    scores = (
        jnp.einsum("rkgd,rskd->rkgs", query_heads, cache_keys, preferred_element_type=jnp.float32)
        * score_scale
    )
    positions = seq_rank * ctx_dev + jnp.arange(ctx_dev, dtype=jnp.int32)
    live_mask = (positions[None, :] < lengths[:, None])[:, None, None, :]
    scores = jnp.where(live_mask, scores, MASKED)
    block_max = jnp.max(scores, axis=3)
    weights = jnp.where(live_mask, jnp.exp(scores - block_max[..., None]), 0.0).astype(jnp.bfloat16)
    block_total = jnp.sum(lax.optimization_barrier(weights).astype(jnp.float32), axis=3)
    block_out = jnp.einsum(
        "rkgs,rskd->rkgd", weights, cache_values, preferred_element_type=jnp.float32
    )
    best_score = lax.pmax(block_max, "seq")
    factor = jnp.exp(block_max - best_score)
    total_weight, gathered = lax.psum((block_total * factor, block_out * factor[..., None]), "seq")
    own_key = new_keyval[:, 0].reshape(row_count, kv_heads, HEAD_DIM)
    own_value = new_keyval[:, 1].reshape(row_count, kv_heads, HEAD_DIM).astype(jnp.float32)
    own_score = (
        jnp.einsum("rkgd,rkd->rkg", query_heads, own_key, preferred_element_type=jnp.float32)
        * score_scale
    )
    top_score = jnp.maximum(best_score, own_score)
    old_weight = jnp.exp(best_score - top_score)
    fresh_weight = jnp.exp(own_score - top_score)
    attended = (
        old_weight[..., None] * gathered + fresh_weight[..., None] * own_value[:, :, None, :]
    ) / (old_weight * total_weight + fresh_weight)[..., None]
    attended = attended.reshape(row_count, q_heads * HEAD_DIM).astype(jnp.bfloat16)
    attend_term = jnp.dot(attended, attend_proj, preferred_element_type=jnp.float32)
    hidden_out = (one_float + lax.psum(attend_term, "tp")).astype(jnp.bfloat16)
    return (hidden_out, new_keyval)


def solution(mesh):
    in_specs = (
        P("grp", "seq"),
        P("seq"),
        P("seq", "tp"),
        P("seq", None, "tp"),
        P("tp", "seq"),
        P(None, "grp", "seq", "tp"),
        P("grp"),
    )
    out_specs = (P("grp", "seq"), P("grp", None, "tp"))
    return jax.shard_map(
        on_device, mesh=mesh, in_specs=in_specs, out_specs=out_specs, check_vma=False
    )
```

profile of v0, /device:TPU:0, one launch (start us, length us, event | category | flops | bytes accessed | tf_op | source)
XLA Modules:
  0.0 106.3 jit_solution(10798045610524827243)
XLA Ops:
  0.6 0.0 copy-start.1
  0.6 0.0 copy-start.2
  0.7 0.0 copy-start
  0.7 1.5 %copy.18 = bf16[128,8,2,256]{3,1,2,0:T(8,128)(2,1)S(1)} copy(bf16[128,8,2,256]{3,2,1,0:T(2,128)(2,1)} %bitcast.46) | data formatting | bytes 2097152
  2.2 0.0 copy-start.3
  2.2 0.5 copy.12
  2.7 0.0 copy-done.1
  2.7 0.0 copy-done.2
  2.7 0.4 fusion.16
  3.1 0.0 copy-done
  3.2 2.8 %fusion.19 = f32[4,2048]{1,0:T(4,128)S(1)} fusion(bf16[1024,2048]{1,0:T(8,128)(2,1)} %param.9, bf16[4,1024]{1,0:T(4,128)(2,1)S(1)} %copy-done.1, f32[1024]{0:T(1024)S(1)} %copy-done.2), kind=kOutput, calls=%fused_computation.30 | convolution fusion | flops 16789504 | bytes 4239360 | tf_op jit(solution)/shard_map/dot_general | solution.py:27
  6.0 0.1 fusion.4
  6.2 39.2 %all-reduce.1 = (f32[4,2048]{1,0:T(4,128)S(1)}, f32[4]{0:T(128)S(1)}) all-reduce(f32[4,2048]{1,0:T(4,128)S(1)} %fusion.19, f32[4]{0:T(128)S(1)} %fusion.4), channel_id=1, replica_groups=mesh['grp'=2,'seq'=8,'tp'=2] {'seq'}, use_global_device_ids=true, to_apply=%region_0.0 | all-reduce | flops 8196 | bytes 65568 | tf_op jit(solution)/shard_map/psum | solution.py:31
  45.3 0.1 fusion.6
  45.4 0.0 copy-done.3
  45.4 0.1 broadcast_compare_fusion
  45.5 0.2 fusion.27
  45.7 0.1 select_convert_fusion
  45.9 0.1 convert_reduce_fusion
  46.0 17.1 %pmax.7 = f32[4,2,8]{2,1,0:T(2,128)S(1)} all-reduce(f32[4,2,8]{2,1,0:T(2,128)S(1)} %get-tuple-element.20), channel_id=1, replica_groups=mesh['grp'=2,'seq'=8,'tp'=2] {'seq'}, use_global_device_ids=true, to_apply=%region_4.5 | all-reduce | flops 64 | bytes 512 | tf_op jit(solution)/shard_map/pmax | solution.py:51
  63.1 0.1 convolution_multiply_fusion
  63.2 35.3 %all-reduce = (f32[4,2,256]{2,0,1:T(4,128)S(1)}, f32[4,2,8]{2,1,0:T(2,128)S(1)}, f32[4,2,8,128]{3,2,1,0:T(8,128)S(1)}) all-reduce(f32[4,2,256]{2,0,1:T(4,128)S(1)} %fusion.16, f32[4,2,8]{2,1,0:T(2,128)S(1)} %bitcast.50, f32[4,2,8,128]{3,2,1,0:T(8,128)S(1)} %convolution_multiply_fusion), channel_id=1, replica_groups=mesh['grp'=2,'seq'=8,'tp'=2] {'seq'}, use_global_device_ids=true, to_apply=%region_5.6 | all-reduce | flops 10304 | bytes 82432 | tf_op jit(solution)/shard_map/psum | solution.py:31
  98.5 0.1 multiply_convert_fusion.1
  98.6 0.1 fusion.10
  98.8 0.1 fusion.13
  98.9 2.8 %fusion.7 = f32[4,1024]{1,0:T(4,128)S(1)} fusion(bf16[2048,1024]{1,0:T(8,128)(2,1)} %param.11, bf16[1,4,16,128]{3,2,1,0:T(8,128)(2,1)S(1)} %fusion.13), kind=kOutput, calls=%fused_computation.16 | convolution fusion | flops 16777216 | bytes 4227072 | tf_op jit(solution)/shard_map/dot_general | solution.py:67
  101.7 3.4 %psum.47 = f32[4,1024]{1,0:T(4,128)S(1)} all-reduce(f32[4,1024]{1,0:T(4,128)S(1)} %fusion.7), channel_id=1, replica_groups=mesh['grp'=2,'seq'=8,'tp'=2] {'tp'}, use_global_device_ids=true, to_apply=%region_9.10 | all-reduce | flops 4096 | bytes 32768 | tf_op jit(solution)/shard_map/psum | solution.py:68
  105.1 0.6 fusion.5
  105.7 0.6 copy.14
  (10 shorter events, 0.2 us)
Async XLA Ops:
  0.6 2.1 %copy-start.1 = (bf16[4,1024]{1,0:T(4,128)(2,1)S(1)}, bf16[4,1024]{1,0:T(4,128)(2,1)}, u32[]{:S(2)}) copy-start(bf16[4,1024]{1,0:T(4,128)(2,1)} %param.7) | copy-start | bytes 24580
  0.6 2.1 %copy-start.2 = (f32[1024]{0:T(1024)S(1)}, f32[1024]{0:T(1024)}, u32[]{:S(2)}) copy-start(f32[1024]{0:T(1024)} %param.8) | copy-start | bytes 12292
  0.7 2.5 %copy-start = (bf16[2,4,64,256]{3,2,1,0:T(8,128)(2,1)S(1)}, bf16[2,4,64,256]{3,2,1,0:T(8,128)(2,1)}, u32[]{:S(2)}) copy-start(bf16[2,4,64,256]{3,2,1,0:T(8,128)(2,1)} %param.12) | copy-start | bytes 786436
  2.2 43.3 %copy-start.3 = (s32[4]{0:T(128)S(1)}, s32[4]{0:T(128)}, u32[]{:S(2)}) copy-start(s32[4]{0:T(128)} %param.13) | copy-start | bytes 52
where the time goes:
time: 107 us; the launch traced here: 106 us
  blocking collectives  94.9 us (89%)
  matrix products  6.52 us (6%)
  local copies, waits for them, and re-layouts  2.77 us (3%)
  other arithmetic  1.3 us (1%)
    psum x2, blocking collectives, on_device(): lax.psum((query_part, keyval_part, squares), 'seq')  74.5 us
    pmax x1, blocking collectives, on_device(): best_score = lax.pmax(block_max, 'seq')  17.1 us
    psum x1, blocking collectives, on_device(): hidden_out = (one_float + lax.psum(attend_term, 'tp')).astype(jnp.bfloat16)  3.35 us
    dot_general x1, matrix products, on_device(): query_part = jnp.dot(scaled, query_proj, preferred_element_type=jnp.float32)  2.84 us
    dot_general x1, matrix products, on_device(): jnp.dot(attended, attend_proj, preferred_element_type=jnp.float32)  2.84 us

commit v1 on v0

--- a/solution.py
+++ b/solution.py
@@ -1,6 +1,10 @@
+import functools
+
 import jax
 import jax.numpy as jnp
 from jax import lax
+from jax.experimental import pallas as pl
+from jax.experimental.pallas import tpu as pltpu
 from jax.sharding import PartitionSpec as P
 
 D = 8192
@@ -69,6 +73,353 @@
     return (hidden_out, new_keyval)
 
 
+MESH = pl.DeviceIdType.MESH
+F32 = jnp.float32
+BF16 = jnp.bfloat16
+QUERY_PIECES = 4
+OUT_PIECES = 4
+
+
+def fused_kernel(
+    n,
+    hidden_ref,
+    gain_ref,
+    lengths_ref,
+    query_hbm,
+    keyval_hbm,
+    attend_hbm,
+    cache_hbm,
+    out_ref,
+    kv_out_ref,
+    query_w,
+    keyval_w,
+    attend_w,
+    cache,
+    sums_out,
+    sums_in,
+    sums_mine,
+    sums_all,
+    soft_out,
+    soft_in,
+    att_mine,
+    att_all,
+    term_mine,
+    term_in,
+    load_sem,
+    send_sem,
+    recv_sem,
+):
+    me = lax.axis_index("seq")
+    core = lax.axis_index("tp")
+    rows, feature_dev = hidden_ref.shape
+    width = query_w.shape[1]
+    q_heads = width // HEAD_DIM
+    ctx_dev = cache.shape[2]
+    kv_heads = cache.shape[3] // HEAD_DIM
+    share = q_heads // kv_heads
+    per = q_heads // n
+    block = per * rows
+    kv_rows = 2 * kv_heads * rows
+    kv_per = kv_rows // n
+    score_scale = HEAD_DIM ** (-0.5)
+
+    step = width // QUERY_PIECES
+    kv_load = pltpu.make_async_copy(keyval_hbm, keyval_w, load_sem.at[0])
+    kv_load.start()
+    query_loads = []
+    for piece in range(QUERY_PIECES):
+        cols = pl.ds(piece * step, step)
+        load = pltpu.make_async_copy(
+            query_hbm.at[:, cols], query_w.at[:, cols], load_sem.at[1 + piece]
+        )
+        load.start()
+        query_loads.append(load)
+    cache_load = pltpu.make_async_copy(cache_hbm, cache, load_sem.at[1 + QUERY_PIECES])
+    cache_load.start()
+    out_loads = []
+    depth = width // OUT_PIECES
+    for piece in range(OUT_PIECES):
+        part = pl.ds(piece * depth, depth)
+        load = pltpu.make_async_copy(
+            attend_hbm.at[part], attend_w.at[part], load_sem.at[2 + QUERY_PIECES + piece]
+        )
+        load.start()
+        out_loads.append(load)
+
+    barrier = pltpu.get_barrier_semaphore()
+    for k in range(1, n):
+        pl.semaphore_signal(
+            barrier, inc=1, device_id={"seq": lax.rem(me + k, n)}, device_id_type=MESH
+        )
+    pl.semaphore_signal(barrier, inc=1, device_id={"tp": 1 - core}, device_id_type=MESH)
+
+    one_float = hidden_ref[...].astype(F32)
+    scaled = one_float * gain_ref[...]
+    scaled_b = scaled.astype(BF16)
+    squares = jnp.sum(one_float * one_float, axis=1, keepdims=True)
+    squares = jnp.broadcast_to(squares, (rows, HEAD_DIM))
+
+    parts = 2 * kv_heads
+    groups = feature_dev // HEAD_DIM
+    span = HEAD_DIM * parts
+    stacked = jnp.concatenate(
+        [scaled[:, g * HEAD_DIM : (g + 1) * HEAD_DIM] for g in range(groups)], axis=0
+    ).astype(BF16)
+    spread_row = lax.broadcasted_iota(jnp.int32, (HEAD_DIM, span), 0)
+    spread_col = lax.broadcasted_iota(jnp.int32, (HEAD_DIM, span), 1)
+    spread = jnp.where(spread_col // parts == spread_row, 1.0, 0.0).astype(BF16)
+    wide = jnp.dot(stacked, spread, preferred_element_type=F32)
+    pick_row = lax.broadcasted_iota(jnp.int32, (kv_rows, span), 0) // rows
+    pick_col = lax.broadcasted_iota(jnp.int32, (kv_rows, span), 1) % parts
+    pick = pick_row == pick_col
+    left = jnp.concatenate(
+        [
+            jnp.where(
+                pick, jnp.concatenate([wide[g * rows : (g + 1) * rows]] * parts, axis=0), 0.0
+            ).astype(BF16)
+            for g in range(groups)
+        ],
+        axis=1,
+    )
+    kv_load.wait()
+    keyval_part = jnp.dot(left, keyval_w[...], preferred_element_type=F32)
+    for c in range(n):
+        sums_out[c, block : block + kv_per, :] = keyval_part[c * kv_per : (c + 1) * kv_per]
+        sums_out[c, block + kv_per : block + kv_per + rows, :] = squares
+
+    for piece in range(QUERY_PIECES):
+        query_loads[piece].wait()
+        product = jnp.dot(
+            scaled_b, query_w[:, piece * step : (piece + 1) * step], preferred_element_type=F32
+        )
+        for h in range(step // HEAD_DIM):
+            head = piece * (step // HEAD_DIM) + h
+            low = (head % per) * rows
+            sums_out[head // per, low : low + rows, :] = product[
+                :, h * HEAD_DIM : (h + 1) * HEAD_DIM
+            ]
+
+    pl.semaphore_wait(barrier, n)
+
+    pending = []
+
+    def send(source, target, phase, k):
+        copy = pltpu.make_async_remote_copy(
+            src_ref=source,
+            dst_ref=target,
+            send_sem=send_sem.at[phase, k],
+            recv_sem=recv_sem.at[phase, k],
+            device_id={"seq": lax.rem(me + k, n)},
+            device_id_type=MESH,
+        )
+        copy.start()
+        pending.append(copy)
+        return copy
+
+    copies = [
+        send(sums_out.at[lax.rem(me + k, n)], sums_in.at[k], 0, k) for k in range(1, n)
+    ]
+    total = sums_out[me]
+    for k in range(1, n):
+        copies[k - 1].wait_recv()
+        total = total + sums_in[k]
+    sums_mine[...] = total
+
+    copies = [send(sums_mine, sums_all.at[me], 1, k) for k in range(1, n)]
+    sums_all[me] = total
+
+    cols = rows * ctx_dev
+    mask_row = lax.broadcasted_iota(jnp.int32, (share * rows, cols), 0) % rows
+    mask_col = lax.broadcasted_iota(jnp.int32, (share * rows, cols), 1)
+    limit = jnp.zeros((share * rows, cols), jnp.int32)
+    for r in range(rows):
+        limit = jnp.where(mask_col // ctx_dev == r, lengths_ref[r], limit)
+    position = me * ctx_dev + mask_col % ctx_dev
+    live = jnp.logical_and(mask_row == mask_col // ctx_dev, position < limit)
+    cache_load.wait()
+
+    for copy in copies:
+        copy.wait_recv()
+    squares_sum = sums_all[0, block + kv_per : block + kv_per + rows, :]
+    scale = lax.rsqrt(squares_sum / (feature_dev * n) + EPSILON)
+    scale_block = jnp.concatenate([scale] * per, axis=0)
+    chunk_heads = share // per
+    lane = lax.broadcasted_iota(jnp.int32, (share * rows, HEAD_DIM), 1)
+    for head in range(kv_heads):
+        query = jnp.concatenate(
+            [
+                sums_all[c, :block, :] * scale_block
+                for c in range(head * chunk_heads, (head + 1) * chunk_heads)
+            ],
+            axis=0,
+        ).astype(BF16)
+        lanes = slice(head * HEAD_DIM, (head + 1) * HEAD_DIM)
+        keys = cache[0, :, :, lanes].reshape(cols, HEAD_DIM)
+        values = cache[1, :, :, lanes].reshape(cols, HEAD_DIM)
+        scores = (
+            lax.dot_general(
+                query, keys, (((1,), (1,)), ((), ())), preferred_element_type=F32
+            )
+            * score_scale
+        )
+        scores = jnp.where(live, scores, MASKED)
+        block_max = jnp.max(scores, axis=1, keepdims=True)
+        weights = jnp.where(live, jnp.exp(scores - block_max), 0.0).astype(BF16)
+        block_total = jnp.sum(weights.astype(F32), axis=1, keepdims=True)
+        block_out = jnp.dot(weights, values, preferred_element_type=F32)
+        stats = jnp.where(lane < HEAD_DIM // 2, block_max, block_total)
+        for c in range(chunk_heads):
+            part = slice(c * block, (c + 1) * block)
+            soft_out[head * chunk_heads + c, :block, :] = block_out[part]
+            soft_out[head * chunk_heads + c, block : 2 * block, :] = stats[part]
+
+    copies = [
+        send(soft_out.at[lax.rem(me + k, n)], soft_in.at[k], 2, k) for k in range(1, n)
+    ]
+
+    keyval = jnp.concatenate(
+        [sums_all[c, block : block + kv_per, :] for c in range(n)], axis=0
+    )
+    keyval = (keyval * jnp.concatenate([scale] * parts, axis=0)).astype(BF16).astype(F32)
+    kv_out_ref[...] = keyval
+    mine = me // chunk_heads
+    own_key = keyval[:rows]
+    own_value = keyval[rows : 2 * rows]
+    for head in range(1, kv_heads):
+        here = mine == head
+        own_key = jnp.where(here, keyval[2 * head * rows : (2 * head + 1) * rows], own_key)
+        own_value = jnp.where(
+            here, keyval[(2 * head + 1) * rows : (2 * head + 2) * rows], own_value
+        )
+    own_key = jnp.concatenate([own_key] * per, axis=0)
+    own_value = jnp.concatenate([own_value] * per, axis=0)
+    query = (sums_all[me, :block, :] * scale_block).astype(BF16).astype(F32)
+    own_score = jnp.sum(query * own_key, axis=1, keepdims=True) * score_scale
+
+    for copy in copies:
+        copy.wait_recv()
+    chunks = [(soft_out[me, :block, :], soft_out[me, block : 2 * block, :])]
+    chunks += [(soft_in[k, :block, :], soft_in[k, block : 2 * block, :]) for k in range(1, n)]
+    maxes = [stats[:, :1] for _, stats in chunks]
+    totals = [stats[:, HEAD_DIM // 2 : HEAD_DIM // 2 + 1] for _, stats in chunks]
+    best = functools.reduce(jnp.maximum, maxes)
+    top = jnp.maximum(best, own_score)
+    fresh = jnp.exp(own_score - top)
+    over = fresh * own_value
+    under = fresh
+    for (values, _), block_max, block_total in zip(chunks, maxes, totals):
+        factor = jnp.exp(block_max - top)
+        over = over + factor * values
+        under = under + factor * block_total
+    attended = (over / under).astype(BF16).astype(F32)
+    att_mine[...] = attended
+
+    copies = [send(att_mine, att_all.at[me], 3, k) for k in range(1, n)]
+    att_all[me] = attended
+    for load in out_loads:
+        load.wait()
+    for copy in copies:
+        copy.wait_recv()
+    attended = jnp.concatenate(
+        [
+            att_all[head // per, (head % per) * rows : (head % per + 1) * rows, :]
+            for head in range(q_heads)
+        ],
+        axis=1,
+    ).astype(BF16)
+    term = jnp.dot(attended, attend_w[...], preferred_element_type=F32)
+    term_mine[...] = term
+    swap = pltpu.make_async_remote_copy(
+        src_ref=term_mine,
+        dst_ref=term_in,
+        send_sem=send_sem.at[0, 0],
+        recv_sem=recv_sem.at[0, 0],
+        device_id={"tp": 1 - core},
+        device_id_type=MESH,
+    )
+    swap.start()
+    for copy in pending:
+        copy.wait_send()
+    swap.wait()
+    out_ref[...] = (one_float + (term + term_in[...])).astype(out_ref.dtype)
+
+
+def fused_device(n, hidden, norm_gain, query_proj, keyval_proj, attend_proj, keyval_cache, lengths):
+    rows, feature_dev = hidden.shape
+    width = query_proj.shape[1]
+    kv_width = keyval_proj.shape[2]
+    kv_heads = kv_width // HEAD_DIM
+    block = width // HEAD_DIM // n * rows
+    kv_rows = 2 * kv_heads * rows
+    chunk = -(-(block + kv_rows // n + rows) // 8) * 8
+    out_width = attend_proj.shape[1]
+    stored = keyval_proj.reshape(feature_dev, 2, kv_heads, HEAD_DIM).transpose(0, 2, 1, 3)
+    stored = stored.reshape(feature_dev * 2 * kv_heads, HEAD_DIM)
+    vmem = pl.BlockSpec(memory_space=pltpu.VMEM)
+    hbm = pl.BlockSpec(memory_space=pl.ANY)
+    hidden_out, keyval = pl.pallas_call(
+        functools.partial(fused_kernel, n),
+        out_shape=(
+            jax.ShapeDtypeStruct((rows, out_width), BF16),
+            jax.ShapeDtypeStruct((kv_rows, HEAD_DIM), F32),
+        ),
+        in_specs=[vmem, vmem, pl.BlockSpec(memory_space=pltpu.SMEM), hbm, hbm, hbm, hbm],
+        out_specs=(vmem, vmem),
+        scratch_shapes=[
+            pltpu.VMEM(query_proj.shape, BF16),
+            pltpu.VMEM(stored.shape, BF16),
+            pltpu.VMEM(attend_proj.shape, BF16),
+            pltpu.VMEM(keyval_cache.shape, BF16),
+            pltpu.VMEM((n, chunk, HEAD_DIM), F32),
+            pltpu.VMEM((n, chunk, HEAD_DIM), F32),
+            pltpu.VMEM((chunk, HEAD_DIM), F32),
+            pltpu.VMEM((n, chunk, HEAD_DIM), F32),
+            pltpu.VMEM((n, 2 * block, HEAD_DIM), F32),
+            pltpu.VMEM((n, 2 * block, HEAD_DIM), F32),
+            pltpu.VMEM((block, HEAD_DIM), F32),
+            pltpu.VMEM((n, block, HEAD_DIM), F32),
+            pltpu.VMEM((rows, out_width), F32),
+            pltpu.VMEM((rows, out_width), F32),
+            pltpu.SemaphoreType.DMA((2 + QUERY_PIECES + OUT_PIECES,)),
+            pltpu.SemaphoreType.DMA((4, n)),
+            pltpu.SemaphoreType.DMA((4, n)),
+        ],
+        compiler_params=pltpu.CompilerParams(collective_id=0, has_side_effects=True),
+    )(
+        hidden,
+        norm_gain.reshape(1, feature_dev),
+        lengths,
+        query_proj,
+        stored,
+        attend_proj,
+        keyval_cache,
+    )
+    new_keyval = keyval.reshape(kv_heads, 2, rows, HEAD_DIM).transpose(2, 1, 0, 3)
+    return hidden_out, new_keyval.reshape(rows, 2, kv_width).astype(BF16)
+
+
+def fits(n, cores, hidden, norm_gain, query_proj, keyval_proj, attend_proj, keyval_cache, lengths):
+    rows, feature_dev = hidden.shape
+    q_heads = query_proj.shape[1] // HEAD_DIM
+    kv_heads = keyval_proj.shape[2] // HEAD_DIM
+    if q_heads % n or (2 * kv_heads * rows) % n or cores != 2 or n < 2:
+        return False
+    per = q_heads // n
+    return (
+        (q_heads // kv_heads) % per == 0
+        and (per * rows) % 8 == 0
+        and feature_dev % HEAD_DIM == 0
+        and keyval_cache.shape[2] % 16 == 0
+        and query_proj.shape[1] % (HEAD_DIM * QUERY_PIECES) == 0
+    )
+
+
+def pick_device(n, cores, *arrays):
+    if fits(n, cores, *arrays):
+        return fused_device(n, *arrays)
+    return on_device(*arrays)
+
+
 def solution(mesh):
     in_specs = (
         P("grp", "seq"),
@@ -80,6 +431,7 @@
         P("grp"),
     )
     out_specs = (P("grp", "seq"), P("grp", None, "tp"))
+    body = functools.partial(pick_device, mesh.shape["seq"], mesh.shape["tp"])
     return jax.shard_map(
-        on_device, mesh=mesh, in_specs=in_specs, out_specs=out_specs, check_vma=False
-    )
+        body, mesh=mesh, in_specs=in_specs, out_specs=out_specs, check_vma=False
+    )

time: 107 us -> 30.8 us (0.29)
  blocking collectives: 94.9 us -> 0 us
  Pallas kernels: 0 us -> 27.2 us
  matrix products: 6.52 us -> 0 us
    psum x3 -> x0, blocking collectives: 77.8 us -> none  [the longest x2 74.5 us: on_device(): lax.psum((query_part, keyval_part, squares), 'seq')]
    pallas_call x0 -> x1, Pallas kernels: none -> 27.2 us  [fused_device(): pl.pallas_call(functools.partial(fused_kernel, n), out_shape=(jax.ShapeDt...]
    pmax x1 -> x0, blocking collectives: 17.1 us -> none  [on_device(): best_score = lax.pmax(block_max, 'seq')]
    dot_general x6 -> x0, matrix products: 6.52 us -> none  [the longest x1 2.84 us: on_device(): query_part = jnp.dot(scaled, query_proj, preferred_element_type=jnp.float32)]
where the time goes in v1:
time: 30.8 us; the launch traced here: 30.4 us
  Pallas kernels  27.2 us (88%)
  local copies, waits for them, and re-layouts  1.91 us (6%)
  other arithmetic  0.7 us (2%)
  between operations  0.64 us (2%)
    pallas_call x1, Pallas kernels, fused_device(): pl.pallas_call(functools.partial(fused_kernel, n), out_shape=(jax.ShapeDt...  27.2 us
    unnamed x1, local copies, waits for them, and re-layouts  1.3 us
    convert_element_type x1, other arithmetic, fused_device(): return (hidden_out, new_keyval.reshape(rows, 2, kv_width).astype(BF16))  0.7 us

profile of v1, /device:TPU:0, one launch (start us, length us, event | category | flops | bytes accessed | tf_op | source)
XLA Modules:
  0.0 30.4 jit_solution(17263134801766099613)
XLA Ops:
  0.6 27.2 %shard_map.86 = (bf16[4,1024]{1,0:T(4,128)(2,1)}, f32[16,128]{1,0:T(8,128)}) custom-call(bf16[4,1024]{1,0:T(4,128)(2,1)} %hidden_ref.1, f32[1,1024]{1,0:T(1,128)} %bitcast.11, s32[4]{0:T(128)} %lengths_ref.1, bf16[1024,2048]{1,0:T(8,128)(2,1)} %query_hbm.1, bf16[4096,128]{1,0:T(8,128)(2,1)} %bitcast.9, bf16[2048,1024]{1,0:T(8,128)(2,1)} %attend_hbm.1, ...), custom_call_target="tpu_custom_call" | custom-call | tf_op jit(solution)/shard_map/pallas_call | solution.py:360
  27.8 0.7 %convert_element_type.12 = bf16[16,128]{1,0:T(8,128)(2,1)S(1)} convert(f32[16,128]{1,0:T(8,128)} %get-tuple-element.5) | non-fusion elementwise | flops 2048 | bytes 12288 | tf_op jit(solution)/shard_map/convert_element_type | solution.py:398
  28.5 0.6 %convert_element_type.15 = bf16[4,2,256]{2,1,0:T(2,128)(2,1)} reshape(bf16[4,2,2,128]{3,2,1,0:T(2,128)(2,1)S(1)} %copy.10) | data formatting | bytes 8192 | tf_op jit(solution)/shard_map/convert_element_type | solution.py:398
  29.1 1.3 %copy.12 = bf16[4,1024]{1,0:T(4,128)(2,1)} copy(bf16[4,1024]{1,0:T(4,128)(2,1)} %get-tuple-element.8) | data formatting | bytes 16384
  (1 shorter events, 0.0 us)

commit v2 on v1

--- a/solution.py
+++ b/solution.py
@@ -82,15 +82,18 @@
 
 def fused_kernel(
     n,
-    hidden_ref,
-    gain_ref,
-    lengths_ref,
+    hidden_hbm,
+    gain_hbm,
+    lengths_hbm,
     query_hbm,
     keyval_hbm,
     attend_hbm,
     cache_hbm,
     out_ref,
     kv_out_ref,
+    hidden_ref,
+    gain_ref,
+    lengths_ref,
     query_w,
     keyval_w,
     attend_w,
@@ -124,6 +127,21 @@
     score_scale = HEAD_DIM ** (-0.5)
 
     step = width // QUERY_PIECES
+    barrier = pltpu.get_barrier_semaphore()
+    for k in range(1, n):
+        pl.semaphore_signal(
+            barrier, inc=1, device_id={"seq": lax.rem(me + k, n)}, device_id_type=MESH
+        )
+    pl.semaphore_signal(barrier, inc=1, device_id={"tp": 1 - core}, device_id_type=MESH)
+
+    small_loads = [
+        pltpu.make_async_copy(source, target, load_sem.at[2 + QUERY_PIECES + OUT_PIECES + i])
+        for i, (source, target) in enumerate(
+            [(hidden_hbm, hidden_ref), (gain_hbm, gain_ref), (lengths_hbm, lengths_ref)]
+        )
+    ]
+    for load in small_loads:
+        load.start()
     kv_load = pltpu.make_async_copy(keyval_hbm, keyval_w, load_sem.at[0])
     kv_load.start()
     query_loads = []
@@ -134,25 +152,8 @@
         )
         load.start()
         query_loads.append(load)
-    cache_load = pltpu.make_async_copy(cache_hbm, cache, load_sem.at[1 + QUERY_PIECES])
-    cache_load.start()
-    out_loads = []
-    depth = width // OUT_PIECES
-    for piece in range(OUT_PIECES):
-        part = pl.ds(piece * depth, depth)
-        load = pltpu.make_async_copy(
-            attend_hbm.at[part], attend_w.at[part], load_sem.at[2 + QUERY_PIECES + piece]
-        )
-        load.start()
-        out_loads.append(load)
-
-    barrier = pltpu.get_barrier_semaphore()
-    for k in range(1, n):
-        pl.semaphore_signal(
-            barrier, inc=1, device_id={"seq": lax.rem(me + k, n)}, device_id_type=MESH
-        )
-    pl.semaphore_signal(barrier, inc=1, device_id={"tp": 1 - core}, device_id_type=MESH)
-
+    for load in small_loads:
+        load.wait()
     one_float = hidden_ref[...].astype(F32)
     scaled = one_float * gain_ref[...]
     scaled_b = scaled.astype(BF16)
@@ -219,6 +220,17 @@
     copies = [
         send(sums_out.at[lax.rem(me + k, n)], sums_in.at[k], 0, k) for k in range(1, n)
     ]
+    cache_load = pltpu.make_async_copy(cache_hbm, cache, load_sem.at[1 + QUERY_PIECES])
+    cache_load.start()
+    out_loads = []
+    depth = width // OUT_PIECES
+    for piece in range(OUT_PIECES):
+        part = pl.ds(piece * depth, depth)
+        load = pltpu.make_async_copy(
+            attend_hbm.at[part], attend_w.at[part], load_sem.at[2 + QUERY_PIECES + piece]
+        )
+        load.start()
+        out_loads.append(load)
     total = sums_out[me]
     for k in range(1, n):
         copies[k - 1].wait_recv()
@@ -281,7 +293,10 @@
         [sums_all[c, block : block + kv_per, :] for c in range(n)], axis=0
     )
     keyval = (keyval * jnp.concatenate([scale] * parts, axis=0)).astype(BF16).astype(F32)
-    kv_out_ref[...] = keyval
+    for head in range(kv_heads):
+        for kind in range(2):
+            low = (2 * head + kind) * rows
+            kv_out_ref[:, kind, head * HEAD_DIM : (head + 1) * HEAD_DIM] = keyval[low : low + rows]
     mine = me // chunk_heads
     own_key = keyval[:rows]
     own_value = keyval[rows : 2 * rows]
@@ -318,16 +333,21 @@
     att_all[me] = attended
     for load in out_loads:
         load.wait()
-    for copy in copies:
-        copy.wait_recv()
-    attended = jnp.concatenate(
-        [
-            att_all[head // per, (head % per) * rows : (head % per + 1) * rows, :]
-            for head in range(q_heads)
-        ],
-        axis=1,
-    ).astype(BF16)
-    term = jnp.dot(attended, attend_w[...], preferred_element_type=F32)
+
+    def project(source):
+        part = att_all[source]
+        part = jnp.concatenate([part[j * rows : (j + 1) * rows] for j in range(per)], axis=1)
+        first = pl.multiple_of(source * (per * HEAD_DIM), per * HEAD_DIM)
+        return jnp.dot(
+            part.astype(BF16),
+            attend_w[pl.ds(first, per * HEAD_DIM), :],
+            preferred_element_type=F32,
+        )
+
+    term = project(me)
+    for k in range(1, n):
+        copies[k - 1].wait_recv()
+        term = term + project(lax.rem(me + n - k, n))
     term_mine[...] = term
     swap = pltpu.make_async_remote_copy(
         src_ref=term_mine,
@@ -360,12 +380,15 @@
     hidden_out, keyval = pl.pallas_call(
         functools.partial(fused_kernel, n),
         out_shape=(
-            jax.ShapeDtypeStruct((rows, out_width), BF16),
-            jax.ShapeDtypeStruct((kv_rows, HEAD_DIM), F32),
+            pltpu.VMEM((rows, out_width), BF16),
+            pltpu.VMEM((rows, 2, kv_width), F32),
         ),
-        in_specs=[vmem, vmem, pl.BlockSpec(memory_space=pltpu.SMEM), hbm, hbm, hbm, hbm],
+        in_specs=[hbm] * 7,
         out_specs=(vmem, vmem),
         scratch_shapes=[
+            pltpu.VMEM(hidden.shape, BF16),
+            pltpu.VMEM((1, feature_dev), F32),
+            pltpu.SMEM(lengths.shape, jnp.int32),
             pltpu.VMEM(query_proj.shape, BF16),
             pltpu.VMEM(stored.shape, BF16),
             pltpu.VMEM(attend_proj.shape, BF16),
@@ -380,7 +403,7 @@
             pltpu.VMEM((n, block, HEAD_DIM), F32),
             pltpu.VMEM((rows, out_width), F32),
             pltpu.VMEM((rows, out_width), F32),
-            pltpu.SemaphoreType.DMA((2 + QUERY_PIECES + OUT_PIECES,)),
+            pltpu.SemaphoreType.DMA((5 + QUERY_PIECES + OUT_PIECES,)),
             pltpu.SemaphoreType.DMA((4, n)),
             pltpu.SemaphoreType.DMA((4, n)),
         ],
@@ -394,8 +417,7 @@
         attend_proj,
         keyval_cache,
     )
-    new_keyval = keyval.reshape(kv_heads, 2, rows, HEAD_DIM).transpose(2, 1, 0, 3)
-    return hidden_out, new_keyval.reshape(rows, 2, kv_width).astype(BF16)
+    return hidden_out, keyval.astype(BF16)
 
 
 def fits(n, cores, hidden, norm_gain, query_proj, keyval_proj, attend_proj, keyval_cache, lengths):

time: 30.8 us -> 27.8 us (0.903)
  Pallas kernels: 27.2 us -> 25.8 us
  local copies, waits for them, and re-layouts: 1.91 us -> 0.6 us
    pallas_call x1, Pallas kernels: 27.2 us -> 25.8 us  [fused_device(): pl.pallas_call(functools.partial(fused_kernel, n), out_shape=(pltpu.VMEM(...]
    unnamed x1, local copies, waits for them, and re-layouts: 1.3 us -> 0.6 us
    convert_element_type x2 -> x0, local copies, waits for them, and re-layouts: 0.61 us -> none  [fused_device(): return (hidden_out, new_keyval.reshape(rows, 2, kv_width).astype(BF16))]
where the time goes in v2:
time: 27.8 us; the launch traced here: 27.6 us
  Pallas kernels  25.8 us (93%)
  between operations  0.64 us (2%)
  local copies, waits for them, and re-layouts  0.6 us (2%)
  other arithmetic  0.6 us (2%)
    pallas_call x1, Pallas kernels, fused_device(): pl.pallas_call(functools.partial(fused_kernel, n), out_shape=(pltpu.VMEM(...  25.8 us
    unnamed x1, local copies, waits for them, and re-layouts  0.6 us
    convert_element_type x1, other arithmetic, fused_device(): return (hidden_out, keyval.astype(BF16))  0.6 us

profile of v2, /device:TPU:0, one launch (start us, length us, event | category | flops | bytes accessed | tf_op | source)
XLA Modules:
  0.0 27.6 jit_solution(12242964599410325190)
XLA Ops:
  0.6 25.8 %shard_map.86 = (bf16[4,1024]{1,0:T(4,128)(2,1)S(1)}, f32[4,2,256]{2,1,0:T(2,128)S(1)}) custom-call(bf16[4,1024]{1,0:T(4,128)(2,1)} %hidden_hbm.1, f32[1,1024]{1,0:T(1,128)} %bitcast.7, s32[4]{0:T(128)} %lengths_hbm.1, bf16[1024,2048]{1,0:T(8,128)(2,1)} %query_hbm.1, bf16[4096,128]{1,0:T(8,128)(2,1)} %bitcast.6, bf16[2048,1024]{1,0:T(8,128)(2,1)} %attend_hbm.1, ...), custom_call_target="tpu_custom_call" | custom-call | tf_op jit(solution)/shard_map/pallas_call | solution.py:380
  26.5 0.6 %copy.11 = bf16[4,1024]{1,0:T(4,128)(2,1)} copy(bf16[4,1024]{1,0:T(4,128)(2,1)S(1)} %get-tuple-element.6) | data formatting | bytes 16384
  27.1 0.6 %convert_element_type.3 = bf16[4,2,256]{2,1,0:T(2,128)(2,1)} convert(f32[4,2,256]{2,1,0:T(2,128)S(1)} %get-tuple-element.5) | non-fusion elementwise | flops 2048 | bytes 12288 | tf_op jit(solution)/shard_map/convert_element_type | solution.py:420

commit v3 on v2

--- a/solution.py
+++ b/solution.py
@@ -204,22 +204,39 @@
 
     pending = []
 
-    def send(source, target, phase, k):
+    upper = (2 * me) // n
+    peers = []
+    for j in range(n - 1):
+        down = n - 1 - j - (me + j + 1) // n
+        up = j + (n + j - me) // n
+        peers.append(down + (up - down) * upper)
+
+    def send(source, target, phase, j):
         copy = pltpu.make_async_remote_copy(
             src_ref=source,
             dst_ref=target,
-            send_sem=send_sem.at[phase, k],
-            recv_sem=recv_sem.at[phase, k],
-            device_id={"seq": lax.rem(me + k, n)},
+            send_sem=send_sem.at[phase, j],
+            recv_sem=recv_sem.at[phase, me],
+            device_id={"seq": peers[j]},
             device_id_type=MESH,
         )
         copy.start()
         pending.append(copy)
-        return copy
-
-    copies = [
-        send(sums_out.at[lax.rem(me + k, n)], sums_in.at[k], 0, k) for k in range(1, n)
-    ]
+
+    def receive(slots, phase, j):
+        pltpu.make_async_remote_copy(
+            src_ref=slots.at[peers[j]],
+            dst_ref=slots.at[peers[j]],
+            send_sem=send_sem.at[phase, j],
+            recv_sem=recv_sem.at[phase, peers[j]],
+            device_id={"seq": peers[j]},
+            device_id_type=MESH,
+        ).wait_recv()
+
+    near_first = list(range(n - 2, -1, -1))
+
+    for j in range(n - 1):
+        send(sums_out.at[peers[j]], sums_in.at[me], 0, j)
     cache_load = pltpu.make_async_copy(cache_hbm, cache, load_sem.at[1 + QUERY_PIECES])
     cache_load.start()
     out_loads = []
@@ -232,12 +249,13 @@
         load.start()
         out_loads.append(load)
     total = sums_out[me]
-    for k in range(1, n):
-        copies[k - 1].wait_recv()
-        total = total + sums_in[k]
+    for j in near_first:
+        receive(sums_in, 0, j)
+        total = total + sums_in[peers[j]]
     sums_mine[...] = total
 
-    copies = [send(sums_mine, sums_all.at[me], 1, k) for k in range(1, n)]
+    for j in range(n - 1):
+        send(sums_mine, sums_all.at[me], 1, j)
     sums_all[me] = total
 
     cols = rows * ctx_dev
@@ -250,8 +268,8 @@
     live = jnp.logical_and(mask_row == mask_col // ctx_dev, position < limit)
     cache_load.wait()
 
-    for copy in copies:
-        copy.wait_recv()
+    for j in near_first:
+        receive(sums_all, 1, j)
     squares_sum = sums_all[0, block + kv_per : block + kv_per + rows, :]
     scale = lax.rsqrt(squares_sum / (feature_dev * n) + EPSILON)
     scale_block = jnp.concatenate([scale] * per, axis=0)
@@ -285,9 +303,8 @@
             soft_out[head * chunk_heads + c, :block, :] = block_out[part]
             soft_out[head * chunk_heads + c, block : 2 * block, :] = stats[part]
 
-    copies = [
-        send(soft_out.at[lax.rem(me + k, n)], soft_in.at[k], 2, k) for k in range(1, n)
-    ]
+    for j in range(n - 1):
+        send(soft_out.at[peers[j]], soft_in.at[me], 2, j)
 
     keyval = jnp.concatenate(
         [sums_all[c, block : block + kv_per, :] for c in range(n)], axis=0
@@ -311,10 +328,10 @@
     query = (sums_all[me, :block, :] * scale_block).astype(BF16).astype(F32)
     own_score = jnp.sum(query * own_key, axis=1, keepdims=True) * score_scale
 
-    for copy in copies:
-        copy.wait_recv()
+    for j in near_first:
+        receive(soft_in, 2, j)
     chunks = [(soft_out[me, :block, :], soft_out[me, block : 2 * block, :])]
-    chunks += [(soft_in[k, :block, :], soft_in[k, block : 2 * block, :]) for k in range(1, n)]
+    chunks += [(soft_in[p, :block, :], soft_in[p, block : 2 * block, :]) for p in peers]
     maxes = [stats[:, :1] for _, stats in chunks]
     totals = [stats[:, HEAD_DIM // 2 : HEAD_DIM // 2 + 1] for _, stats in chunks]
     best = functools.reduce(jnp.maximum, maxes)
@@ -329,7 +346,8 @@
     attended = (over / under).astype(BF16).astype(F32)
     att_mine[...] = attended
 
-    copies = [send(att_mine, att_all.at[me], 3, k) for k in range(1, n)]
+    for j in range(n - 1):
+        send(att_mine, att_all.at[me], 3, j)
     att_all[me] = attended
     for load in out_loads:
         load.wait()
@@ -345,15 +363,15 @@
         )
 
     term = project(me)
-    for k in range(1, n):
-        copies[k - 1].wait_recv()
-        term = term + project(lax.rem(me + n - k, n))
+    for j in near_first:
+        receive(att_all, 3, j)
+        term = term + project(peers[j])
     term_mine[...] = term
     swap = pltpu.make_async_remote_copy(
         src_ref=term_mine,
         dst_ref=term_in,
-        send_sem=send_sem.at[0, 0],
-        recv_sem=recv_sem.at[0, 0],
+        send_sem=send_sem.at[4, 0],
+        recv_sem=recv_sem.at[4, 0],
         device_id={"tp": 1 - core},
         device_id_type=MESH,
     )
@@ -404,8 +422,8 @@
             pltpu.VMEM((rows, out_width), F32),
             pltpu.VMEM((rows, out_width), F32),
             pltpu.SemaphoreType.DMA((5 + QUERY_PIECES + OUT_PIECES,)),
-            pltpu.SemaphoreType.DMA((4, n)),
-            pltpu.SemaphoreType.DMA((4, n)),
+            pltpu.SemaphoreType.DMA((5, n)),
+            pltpu.SemaphoreType.DMA((5, n)),
         ],
         compiler_params=pltpu.CompilerParams(collective_id=0, has_side_effects=True),
     )(

time: 27.8 us -> 26.6 us (0.957)
  Pallas kernels: 25.8 us -> 24.6 us
    pallas_call x1, Pallas kernels: 25.8 us -> 24.6 us  [fused_device(): pl.pallas_call(functools.partial(fused_kernel, n), out_shape=(pltpu.VMEM(...]
where the time goes in v3:
time: 26.6 us; the launch traced here: 26.4 us
  Pallas kernels  24.6 us (92%)
  between operations  0.64 us (2%)
  local copies, waits for them, and re-layouts  0.6 us (2%)
  other arithmetic  0.6 us (2%)
    pallas_call x1, Pallas kernels, fused_device(): pl.pallas_call(functools.partial(fused_kernel, n), out_shape=(pltpu.VMEM(...  24.6 us
    unnamed x1, local copies, waits for them, and re-layouts  0.6 us
    convert_element_type x1, other arithmetic, fused_device(): return (hidden_out, keyval.astype(BF16))  0.6 us

profile of v3, /device:TPU:0, one launch (start us, length us, event | category | flops | bytes accessed | tf_op | source)
XLA Modules:
  0.0 26.4 jit_solution(1416627870367519765)
XLA Ops:
  0.6 24.6 %shard_map.86 = (bf16[4,1024]{1,0:T(4,128)(2,1)S(1)}, f32[4,2,256]{2,1,0:T(2,128)S(1)}) custom-call(bf16[4,1024]{1,0:T(4,128)(2,1)} %hidden_hbm.1, f32[1,1024]{1,0:T(1,128)} %bitcast.7, s32[4]{0:T(128)} %lengths_hbm.1, bf16[1024,2048]{1,0:T(8,128)(2,1)} %query_hbm.1, bf16[4096,128]{1,0:T(8,128)(2,1)} %bitcast.6, bf16[2048,1024]{1,0:T(8,128)(2,1)} %attend_hbm.1, ...), custom_call_target="tpu_custom_call" | custom-call | tf_op jit(solution)/shard_map/pallas_call | solution.py:398
  25.2 0.6 %copy.11 = bf16[4,1024]{1,0:T(4,128)(2,1)} copy(bf16[4,1024]{1,0:T(4,128)(2,1)S(1)} %get-tuple-element.6) | data formatting | bytes 16384
  25.8 0.6 %convert_element_type.3 = bf16[4,2,256]{2,1,0:T(2,128)(2,1)} convert(f32[4,2,256]{2,1,0:T(2,128)S(1)} %get-tuple-element.5) | non-fusion elementwise | flops 2048 | bytes 12288 | tf_op jit(solution)/shard_map/convert_element_type | solution.py:438
